TPU v7x, 128 devices: a whole 4x4x4 slice. The times are simulated.
128 devices in a mesh: dp: 4 (over z), mp: 32 (over y, x, core).
Axes of the slice: x: 4, y: 4, z: 4, core: 2. Of those that a mesh axis runs over, the one named last changes fastest.
Arguments:
- tokens: bfloat16 [4096, 4096], P('dp', 'mp'), may hold values from -6 to 6
- decay: float32 [4096, 16], P('dp'), may hold values from 0.75 to 1, as said below
- state: float32 [128, 256, 8192], P('dp', None, 'mp'), may hold values from -24 to 24
- w_query: bfloat16 [4096, 4096], P(None, 'mp'), may hold values from -0.09375 to 0.09375
- w_key: bfloat16 [4096, 4096], P(None, 'mp'), may hold values from -0.09375 to 0.09375
- w_value: bfloat16 [4096, 8192], P(None, 'mp'), may hold values from -0.09375 to 0.09375
- w_gate: bfloat16 [4096, 8192], P(None, 'mp'), may hold values from -0.09375 to 0.09375
- w_out: bfloat16 [8192, 4096], P('mp'), may hold values from -0.125 to 0.125
- norm_gain: float32 [8192], P('mp'), may hold values from 0.25 to 1.75
Outputs:
- layer_out: bfloat16 [4096, 4096], P('dp', 'mp')
- new_state: float32 [128, 256, 8192], P('dp', None, 'mp')
Inputs may be any that keep to these rules, and one draw needn't show every extreme that they name: `decay`: each head has its own base rate over all tokens, varied somewhat from token to token.
All inputs are finite; a program needn't handle non-finite values.
Results may differ from a plain program's by a relative error of at most 0.0071.
Values may be sent and summed in bfloat16 or wider, within the bound.
No kernel may reach another device: no remote copies, remote signals or barrier semaphores. Data moves between devices by JAX's collectives and lax.ppermute only.
A program may use at most 128 MiB of HBM per device.

v0:
```python
import jax
import jax.numpy as jnp
from jax import lax
from jax.sharding import PartitionSpec as P

HEAD = 256
VHEAD = 512
NEW = 32
EPS = 0.1


def partner(shard, axis, bit):
    return lax.ppermute(shard, axis, [(i, i ^ 1 << bit) for i in range(lax.axis_size(axis))])


def per_device(tokens, decay, state, w_query, w_key, w_value, w_gate, w_out, norm_gain):
    tok_rows = tokens.shape[0]
    qk_columns = w_query.shape[1]
    v_columns = w_value.shape[1]
    groups = max(1, qk_columns // HEAD)
    qk_width = qk_columns // groups
    v_width = v_columns // groups
    sequences = tok_rows // NEW
    device_index = lax.axis_index("mp")
    first_head = device_index * qk_columns // HEAD
    qk_zeros = jnp.zeros((tok_rows, qk_columns), jnp.float32)
    v_zeros = jnp.zeros((tok_rows, v_columns), jnp.float32)
    carried = (qk_zeros, qk_zeros, v_zeros, v_zeros)
    segment = lax.all_gather(tokens, "mp", axis=1, tiled=True)
    updated = []
    for running, weight in zip(carried, (w_query, w_key, w_value, w_gate)):
        weight_rows = weight
        updated.append(jnp.dot(segment, weight_rows, preferred_element_type=jnp.float32))
    query, key_proj, value_proj, gate_proj = tuple(updated)
    query = (query * HEAD ** (-0.5)).astype(jnp.bfloat16).reshape(tok_rows, groups, qk_width)
    key_proj = key_proj.astype(jnp.bfloat16).reshape(tok_rows, groups, qk_width)
    value_proj = value_proj.astype(jnp.bfloat16)
    bit_number = 0
    other_query, other_key = partner((query, key_proj), "mp", bit_number)
    upper_half = device_index >> bit_number & 1 == 1
    query = jnp.where(
        upper_half,
        jnp.concatenate([other_query, query], 2),
        jnp.concatenate([query, other_query], 2),
    )
    key_proj = jnp.where(
        upper_half,
        jnp.concatenate([other_key, key_proj], 2),
        jnp.concatenate([key_proj, other_key], 2),
    )
    query_block = query.reshape(sequences, NEW, groups, HEAD)
    key_block = key_proj.reshape(sequences, NEW, groups, HEAD)
    value_block = value_proj.reshape(sequences, NEW, groups, v_width)
    decay_rates = lax.dynamic_slice_in_dim(decay, first_head, groups, 1).reshape(
        sequences, NEW, groups
    )
    log_cumul = jnp.cumsum(jnp.log(decay_rates), axis=1)
    old_state = state.reshape(sequences, HEAD, groups, v_width)
    from_state = jnp.einsum("bngk,bkgv->bngv", query_block.astype(jnp.float32), old_state)
    scores = jnp.einsum(
        "bngk,bmgk->bgnm", query_block, key_block, preferred_element_type=jnp.float32
    )
    along = jnp.transpose(log_cumul, (0, 2, 1))
    log_gap = along[:, :, :, None] - along[:, :, None, :]
    causal = jnp.arange(NEW)[:, None] >= jnp.arange(NEW)[None, :]
    factor = jnp.where(causal, jnp.exp(jnp.where(causal, log_gap, 0.0)), 0.0)
    weights = (scores * factor).astype(jnp.bfloat16)
    in_block = jnp.einsum(
        "bgnm,bmgv->bngv", weights, value_block, preferred_element_type=jnp.float32
    )
    retained = jnp.exp(log_cumul)[..., None] * from_state + in_block
    final_log = log_cumul[:, -1, :]
    carry_scale = jnp.exp(final_log[:, None, :] - log_cumul)
    decayed_keys = key_block.astype(jnp.float32) * carry_scale[..., None]
    fresh = jnp.einsum("bngk,bngv->bkgv", decayed_keys, value_block.astype(jnp.float32))
    new_state = jnp.exp(final_log)[:, None, :, None] * old_state + fresh
    new_state = new_state.reshape(sequences, HEAD, v_columns)
    retained = retained.reshape(tok_rows, groups, v_width)
    running = jnp.sum(retained, axis=-1)
    squares = jnp.sum(retained * retained, axis=-1)
    bit_number = 0
    other_sum, other_square = partner((running, squares), "mp", bit_number)
    running = running + other_sum
    squares = squares + other_square
    centre = running / VHEAD
    variance = squares / VHEAD - centre * centre
    deviation = retained - centre[..., None]
    normed = deviation * lax.rsqrt(variance + EPS)[..., None]
    gated_out = (normed.reshape(tok_rows, v_columns) * norm_gain * jax.nn.silu(gate_proj)).astype(
        jnp.bfloat16
    )
    out_cols = lax.all_to_all(w_out, "mp", split_axis=1, concat_axis=0, tiled=True)
    weight_rows = out_cols
    layer_out = jnp.dot(
        lax.all_gather(gated_out, "mp", axis=1, tiled=True),
        weight_rows,
        preferred_element_type=jnp.float32,
    ).astype(jnp.bfloat16)
    return (layer_out, new_state)


def solution(mesh):
    placed = (
        P("dp", "mp"),
        P("dp", None),
        P("dp", None, "mp"),
        P(None, "mp"),
        P(None, "mp"),
        P(None, "mp"),
        P(None, "mp"),
        P("mp", None),
        P("mp"),
    )
    return jax.shard_map(
        per_device,
        mesh=mesh,
        in_specs=placed,
        out_specs=(P("dp", "mp"), P("dp", None, "mp")),
        check_vma=False,
    )
```

profile of v0, /device:TPU:1, one launch (start us, length us, event | category | flops | bytes accessed | tf_op | source)
XLA Modules:
  0.0 216.4 jit_solution(17912909884485674575)
XLA Ops:
  7.2 0.0 copy-start
  7.2 0.0 all-gather.3.cloned.1.call-start
  7.2 0.7 all-gather.3.cloned.1.call-update
  7.9 0.0 all-gather.5.cloned.1.call-start
  8.0 0.8 log_reduce_fusion
  8.8 0.1 log.15
  8.8 0.5 copy.22
  9.4 2.0 fusion.26
  11.4 0.4 copy.23
  11.7 0.1 slice_reduce_fusion
  11.9 0.1 subtract_exponential_fusion
  11.9 60.5 %all-gather.3.cloned.1.call-done = bf16[1024,4096]{1,0:T(8,128)(2,1)} async-done(((bf16[1024,128]{1,0:T(8,128)(2,1)}), bf16[1024,4096]{1,0:T(8,128)(2,1)}) %all-gather.3.cloned.1.call-update) | async-done | bytes 8388624 | tf_op jit(solution)/shard_map/all_gather | solution.py:29
  72.5 0.0 copy-start.10
  72.5 0.0 copy-start.11
  72.5 6.1 %fusion.4 = bf16[1024,128]{1,0:T(8,128)(2,1)S(1)} fusion(bf16[1024,4096]{1,0:T(8,128)(2,1)} %all-gather.3.cloned.1.call-done, bf16[4096,128]{1,0:T(8,128)(2,1)} %param.12), kind=kOutput, calls=%fused_computation.11 | convolution fusion | flops 1074003968 | bytes 9699328 | tf_op jit(solution)/shard_map/dot_general | solution.py:33
  78.5 0.3 collective-permute-start
  78.9 0.0 copy-done.10
  78.9 0.0 copy-done.11
  78.9 2.3 %convolution_convert_fusion.2 = bf16[1024,128]{1,0:T(8,128)(2,1)S(1)} fusion(bf16[1024,4096]{1,0:T(8,128)(2,1)S(1)} %copy-done.10, bf16[4096,128]{1,0:T(8,128)(2,1)S(1)} %copy-done.11), kind=kOutput, calls=%fused_computation.12 | convolution fusion | flops 1073872896 | bytes 9699328 | tf_op jit(solution)/shard_map/dot_general | solution.py:33
  81.2 0.0 copy-start.6
  81.2 0.3 collective-permute-start.1
  81.6 0.0 copy-done
  81.6 2.3 %convolution_convert_fusion = bf16[1024,256]{1,0:T(8,128)(2,1)S(1)} fusion(bf16[1024,4096]{1,0:T(8,128)(2,1)S(1)} %copy-done.10, bf16[4096,256]{1,0:T(8,128)(2,1)S(1)} %copy-done), kind=kOutput, calls=%fused_computation.6 | convolution fusion | flops 2147745792 | bytes 11010048 | tf_op jit(solution)/shard_map/dot_general | solution.py:33
  83.9 0.0 copy-start.3
  83.9 0.0 collective-permute-done
  83.9 0.0 copy-start.5
  83.9 0.0 collective-permute-done.1
  84.0 0.0 copy-start.8
  84.0 0.8 copy-done.8
  84.7 0.0 copy-start.12
  84.7 1.5 convolution_bitcast_fusion
  86.3 0.0 copy-done.6
  86.3 0.0 copy-done.3
  86.3 0.0 copy-done.5
  86.3 4.5 %fusion.9 = (f32[32,32]{1,0:T(8,128)S(1)}, f32[32,32]{1,0:T(8,128)S(1)}, f32[32,1,256,32]{2,3,0,1:T(8,128)S(1)}) fusion(f32[32,1,256,32]{2,3,0,1:T(8,128)S(1)} %convolution_bitcast_fusion, f32[32,256,256]{2,1,0:T(8,128)} %param.11, bf16[32,32,128]{2,1,0:T(8,128)(2,1)S(1)} %bitcast.72, bf16[32,32,128]{2,1,0:T(8,128)(2,1)} %bitcast.74, pred[]{:T(512)S(6)} %eq.3, ...), kind=kOutput, calls=%fused_computation.20 | convolution fusion | flops 137885696 | bytes 11022337 | tf_op jit(solution)/shard_map/bngk,bkgv->bngv/dot_general | solution.py:59
  90.8 0.1 reduce_sum.25
  90.9 0.1 reduce_sum.23
  91.0 0.3 collective-permute-start.2
  91.3 0.2 collective-permute-start.3
  91.5 0.7 collective-permute-done.2
  92.2 0.3 collective-permute-done.3
  92.5 0.0 copy-done.12
  92.5 0.0 copy-start.2
  92.5 7.4 %fusion.8 = bf16[1024,256]{1,0:T(8,128)(2,1)} fusion(f32[32,1,256,32]{2,3,0,1:T(8,128)S(1)} %get-tuple-element.14, f32[256]{0:T(256)S(1)} %copy-done.12, f32[1024]{0:T(1024)S(1)} %bitcast.81, f32[1024]{0:T(1024)S(1)} %bitcast.82, bf16[1024,4096]{1,0:T(8,128)(2,1)} %all-gather.3.cloned.1.call-done, bf16[4096,256]{1,0:T(8,128)(2,1)} %param.15), kind=kOutput, calls=%fused_computation.17 | convolution fusion | flops 2149842944 | bytes 12067840 | tf_op jit(solution)/shard_map/dot_general | solution.py:33
  99.9 0.0 all-gather.5.cloned.1.call-update
  99.9 0.0 copy-done.2
  99.9 2.5 %copy.24 = bf16[256,4096]{0,1:T(8,128)(2,1)} copy(bf16[256,4096]{1,0:T(8,128)(2,1)S(1)} %copy-done.2) | data formatting | bytes 4194304 | tf_op args[7]
  102.4 5.6 %all-to-all-start = ((bf16[256,32,128]{0,2,1:T(8,128)(2,1)}), bf16[256,32,128]{0,2,1:T(8,128)(2,1)S(1)}, u32[]{:S(2)}, u32[]{:S(2)}) async-start(bf16[256,32,128]{0,2,1:T(8,128)(2,1)} %bitcast.66), calls=%async_computation | async-start | bytes 4194304 | tf_op jit(solution)/shard_map/all_to_all | solution.py:92
  108.0 0.0 copy-start.4
  108.0 0.0 copy-start.7
  108.0 0.0 copy-start.9
  108.0 9.2 %copy.26 = f32[32,256,256]{1,2,0:T(8,128)} copy(f32[32,256,256]{2,1,0:T(8,128)} %param.11) | data formatting | bytes 16777216 | tf_op args[2]
  117.2 27.7 %all-to-all-done = bf16[256,32,128]{0,2,1:T(8,128)(2,1)S(1)} async-done(((bf16[256,32,128]{0,2,1:T(8,128)(2,1)}), bf16[256,32,128]{0,2,1:T(8,128)(2,1)S(1)}, u32[]{:S(2)}, u32[]{:S(2)}) %all-to-all-start) | async-done | bytes 2097184 | tf_op jit(solution)/shard_map/all_to_all | solution.py:92
  144.9 2.9 %copy.25 = bf16[32,256,128]{2,1,0:T(8,128)(2,1)} copy(bf16[32,256,128]{1,2,0:T(8,128)(2,1)S(1)} %bitcast.65) | data formatting | bytes 4194304 | tf_op jit(solution)/shard_map/all_to_all | solution.py:92
  147.8 0.0 copy-done.4
  147.8 0.0 copy-done.7
  147.8 0.0 copy-done.9
  147.8 8.5 %fusion = f32[32,256,256]{1,2,0:T(8,128)} fusion(f32[32,256,256]{1,2,0:T(8,128)} %copy.26, f32[32]{0:T(128)S(1)} %exp.38, bf16[32,32,256]{2,1,0:T(8,128)(2,1)S(1)} %bitcast.69, f32[32,32]{1,0:T(8,128)S(1)} %get-tuple-element.12, bf16[32,32,128]{2,1,0:T(8,128)(2,1)S(1)} %bitcast.77, bf16[32,32,128]{2,1,0:T(8,128)(2,1)S(1)} %bitcast.79, pred[]{:T(512)S(6)} %eq.3), kind=kOutput, calls=%fused_computation.1 | convolution fusion | flops 141295616 | bytes 17830016 | tf_op jit(solution)/shard_map/bngk,bngv->bkgv/dot_general | solution.py:75
  156.3 9.0 %copy.27 = f32[32,256,256]{2,1,0:T(8,128)} copy(f32[32,256,256]{1,2,0:T(8,128)} %fusion) | data formatting | bytes 16777216
  165.3 32.6 %all-gather.5.cloned.1.call-done = bf16[1024,8192]{1,0:T(8,128)(2,1)} async-done(((bf16[1024,256]{1,0:T(8,128)(2,1)}), bf16[1024,8192]{1,0:T(8,128)(2,1)}) %all-gather.5.cloned.1.call-update) | async-done | bytes 16777232 | tf_op jit(solution)/shard_map/all_gather | solution.py:95
  197.9 0.0 copy-start.1
  197.9 11.7 %convolution_convert_fusion.1 = bf16[1024,128]{1,0:T(8,128)(2,1)} fusion(bf16[1024,8192]{1,0:T(8,128)(2,1)} %all-gather.5.cloned.1.call-done, bf16[8192,128]{1,0:T(8,128)(2,1)} %bitcast.67), kind=kOutput, calls=%fused_computation.9 | convolution fusion | flops 2147614720 | bytes 19136512 | tf_op jit(solution)/shard_map/dot_general | solution.py:94
  209.6 0.0 copy-done.1
  (3 shorter events, 0.0 us)
Async XLA Ops:
  7.2 74.4 %copy-start = (bf16[4096,256]{1,0:T(8,128)(2,1)S(1)}, bf16[4096,256]{1,0:T(8,128)(2,1)}, u32[]{:S(2)}) copy-start(bf16[4096,256]{1,0:T(8,128)(2,1)} %param.14) | copy-start | bytes 6291460
  7.2 65.3 %all-gather.3.cloned.1.call-start = ((), (), s32[]{:S(2)}) async-start(), calls=%async_computation.1 | async-start | bytes 8650752 | tf_op jit(solution)/shard_map/all_gather | solution.py:29
  7.9 190.0 %all-gather.5.cloned.1.call-start = ((), (), s32[]{:S(2)}) async-start(), calls=%async_computation.2 | async-start | bytes 17301504 | tf_op jit(solution)/shard_map/all_gather | solution.py:95
  72.5 6.4 %copy-start.10 = (bf16[1024,4096]{1,0:T(8,128)(2,1)S(1)}, bf16[1024,4096]{1,0:T(8,128)(2,1)}, u32[]{:S(2)}) copy-start(bf16[1024,4096]{1,0:T(8,128)(2,1)} %all-gather.3.cloned.1.call-done) | copy-start | bytes 25165828
  72.5 6.4 %copy-start.11 = (bf16[4096,128]{1,0:T(8,128)(2,1)S(1)}, bf16[4096,128]{1,0:T(8,128)(2,1)}, u32[]{:S(2)}) copy-start(bf16[4096,128]{1,0:T(8,128)(2,1)} %param.13) | copy-start | bytes 3145732
  78.5 5.4 %collective-permute-start = (bf16[1024,1,128]{2,0,1:T(8,128)(2,1)S(1)}, bf16[1024,1,128]{2,0,1:T(8,128)(2,1)S(1)}, u32[]{:S(2)}, u32[]{:S(2)}) collective-permute-start(bf16[1024,1,128]{2,0,1:T(8,128)(2,1)S(1)} %bitcast.70), channel_id=1, source_target_pairs={{0,1},{1,0},{2,3},{3,2},{4,5},{5,4},{6,7},{7,6},{8,9},{9,8},{10,11... | collective-permute-start | bytes 786440 | tf_op jit(solution)/shard_map/ppermute | solution.py:13
  81.2 5.0 %copy-start.6 = (bf16[1024,128]{1,0:T(8,128)(2,1)}, bf16[1024,128]{1,0:T(8,128)(2,1)S(1)}, u32[]{:S(2)}) copy-start(bf16[1024,128]{1,0:T(8,128)(2,1)S(1)} %convolution_convert_fusion.2) | copy-start | bytes 786436
  81.2 2.7 %collective-permute-start.1 = (bf16[1024,1,128]{2,0,1:T(8,128)(2,1)S(1)}, bf16[1024,1,128]{2,0,1:T(8,128)(2,1)S(1)}, u32[]{:S(2)}, u32[]{:S(2)}) collective-permute-start(bf16[1024,1,128]{2,0,1:T(8,128)(2,1)S(1)} %bitcast.75), channel_id=1, source_target_pairs={{0,1},{1,0},{2,3},{3,2},{4,5},{5,4},{6,7},{7,6},{8,9},{9,8},{10,11... | collective-permute-start | bytes 786440 | tf_op jit(solution)/shard_map/ppermute | solution.py:13
  83.9 2.4 %copy-start.3 = (bf16[1024,256]{1,0:T(8,128)(2,1)}, bf16[1024,256]{1,0:T(8,128)(2,1)S(1)}, u32[]{:S(2)}) copy-start(bf16[1024,256]{1,0:T(8,128)(2,1)S(1)} %convolution_convert_fusion) | copy-start | bytes 1572868
  83.9 2.4 %copy-start.5 = (bf16[1024,1,128]{2,0,1:T(8,128)(2,1)}, bf16[1024,1,128]{2,0,1:T(8,128)(2,1)S(1)}, u32[]{:S(2)}) copy-start(bf16[1024,1,128]{2,0,1:T(8,128)(2,1)S(1)} %collective-permute-done) | copy-start | bytes 786436
  84.0 0.8 copy-start.8
  84.7 7.8 %copy-start.12 = (f32[256]{0:T(256)S(1)}, f32[256]{0:T(256)}, u32[]{:S(2)}) copy-start(f32[256]{0:T(256)} %param.17) | copy-start | bytes 3076
  91.0 1.2 collective-permute-start.2
  91.3 1.2 collective-permute-start.3
  92.5 7.4 %copy-start.2 = (bf16[256,4096]{1,0:T(8,128)(2,1)S(1)}, bf16[256,4096]{1,0:T(8,128)(2,1)}, u32[]{:S(2)}) copy-start(bf16[256,4096]{1,0:T(8,128)(2,1)} %param.16) | copy-start | bytes 6291460
  102.4 42.5 %all-to-all-start = ((bf16[256,32,128]{0,2,1:T(8,128)(2,1)}), bf16[256,32,128]{0,2,1:T(8,128)(2,1)S(1)}, u32[]{:S(2)}, u32[]{:S(2)}) async-start(bf16[256,32,128]{0,2,1:T(8,128)(2,1)} %bitcast.66), calls=%async_computation | async-start | bytes 4194304 | tf_op jit(solution)/shard_map/all_to_all | solution.py:92
  108.0 39.8 %copy-start.4 = (bf16[1024,256]{1,0:T(8,128)(2,1)S(1)}, bf16[1024,256]{1,0:T(8,128)(2,1)}, u32[]{:S(2)}) copy-start(bf16[1024,256]{1,0:T(8,128)(2,1)} %copy-done.3) | copy-start | bytes 1572868
  108.0 39.8 %copy-start.7 = (bf16[1024,128]{1,0:T(8,128)(2,1)S(1)}, bf16[1024,128]{1,0:T(8,128)(2,1)}, u32[]{:S(2)}) copy-start(bf16[1024,128]{1,0:T(8,128)(2,1)} %copy-done.6) | copy-start | bytes 786436
  108.0 39.8 %copy-start.9 = (bf16[1024,1,128]{2,0,1:T(8,128)(2,1)S(1)}, bf16[1024,1,128]{2,0,1:T(8,128)(2,1)}, u32[]{:S(2)}) copy-start(bf16[1024,1,128]{2,0,1:T(8,128)(2,1)} %copy-done.8) | copy-start | bytes 786436
  197.9 11.7 %copy-start.1 = (bf16[4096,256]{1,0:T(8,128)(2,1)S(1)}, bf16[4096,256]{1,0:T(8,128)(2,1)}, u32[]{:S(2)}) copy-start(bf16[4096,256]{1,0:T(8,128)(2,1)} %param.14) | copy-start | bytes 6291460
Sparse Core Ops, SparseCore 0:
  10.2 62.2 all-gather.2
  100.0 97.8 all-gather.4
where the time goes:
time: 217 us; the launch traced here: 216 us
  waiting for transfers between devices  122 us (56%)
  matrix products  44.4 us (20%)
  local copies, waits for them, and re-layouts  26.4 us (12%)
  between operations  14.3 us (7%)
  starting transfers between devices  6.87 us (3%)
    all_gather x1, waiting for transfers between devices, per_device(): segment = lax.all_gather(tokens, 'mp', axis=1, tiled=True)  60.5 us
    all_gather x1, waiting for transfers between devices, per_device(): lax.all_gather(gated_out, 'mp', axis=1, tiled=True)  32.6 us
    all_to_all x1, waiting for transfers between devices, per_device(): lax.all_to_all(w_out, 'mp', split_axis=1, concat_axis=0, tiled=True)  27.7 us
    unnamed x29, local copies, waits for them, and re-layouts  21.5 us
    dot_general x4, matrix products, per_device(): jnp.dot(segment, weight_rows, preferred_element_type=jnp.float32)  18.1 us
    dot_general x1, matrix products, per_device(): jnp.dot(lax.all_gather(gated_out, 'mp', axis=1, tiled=True), weight_rows,...  11.7 us
    dot_general x1, matrix products, per_device(): jnp.einsum('bngk,bngv->bkgv', decayed_keys, value_block.astype(jnp.float32))  8.48 us
    all_to_all x1, starting transfers between devices, per_device(): lax.all_to_all(w_out, 'mp', split_axis=1, concat_axis=0, tiled=True)  5.6 us
  transfers between devices with their start and end apart: 7, of which 5 were waited for; matrix products, arithmetic and copies ran while one was open for 19% of the time, Pallas kernels for 0%

commit v1 on v0

--- a/solution.py
+++ b/solution.py
@@ -7,6 +7,14 @@
 VHEAD = 512
 NEW = 32
 EPS = 0.1
+
+
+def gather_by_exchange(value, axis, dim):
+    count = lax.axis_size(axis)
+    repeats = [count if d == dim else 1 for d in range(value.ndim)]
+    return lax.all_to_all(
+        jnp.tile(value, repeats), axis, split_axis=dim, concat_axis=dim, tiled=True
+    )
 
 
 def partner(shard, axis, bit):
@@ -92,9 +100,7 @@
     out_cols = lax.all_to_all(w_out, "mp", split_axis=1, concat_axis=0, tiled=True)
     weight_rows = out_cols
     layer_out = jnp.dot(
-        lax.all_gather(gated_out, "mp", axis=1, tiled=True),
-        weight_rows,
-        preferred_element_type=jnp.float32,
+        gather_by_exchange(gated_out, "mp", 1), weight_rows, preferred_element_type=jnp.float32
     ).astype(jnp.bfloat16)
     return (layer_out, new_state)
 

time: 217 us -> 360 us (1.66)
  the two profiles are of different devices: /device:TPU:1 before, /device:TPU:0 now
where the time goes in v1:
time: 360 us; the launch traced here: 359 us
  waiting for transfers between devices  250 us (69%)
  matrix products  42.6 us (12%)
  local copies, waits for them, and re-layouts  34.9 us (10%)
  starting transfers between devices  14.7 us (4%)
  between operations  14.2 us (4%)
    all_to_all x1, waiting for transfers between devices, gather_by_exchange(): lax.all_to_all(jnp.tile(value, repeats), axis, split_axis=dim, concat_axi...  187 us
    all_gather x1, waiting for transfers between devices, per_device(): segment = lax.all_gather(tokens, 'mp', axis=1, tiled=True)  61.6 us
    unnamed x17, local copies, waits for them, and re-layouts  22.9 us
    dot_general x4, matrix products, per_device(): jnp.dot(segment, weight_rows, preferred_element_type=jnp.float32)  17.2 us
    dot_general x1, matrix products, per_device(): jnp.dot(gather_by_exchange(gated_out, 'mp', 1), weight_rows, preferred_el...  11.6 us
    dot_general x1, matrix products, per_device(): jnp.einsum('bngk,bngv->bkgv', decayed_keys, value_block.astype(jnp.float32))  7.98 us
    all_to_all x1, starting transfers between devices, per_device(): lax.all_to_all(w_out, 'mp', split_axis=1, concat_axis=0, tiled=True)  7.56 us
  transfers between devices with their start and end apart: 7, of which 4 were waited for; matrix products, arithmetic and copies ran while one was open for 17% of the time, Pallas kernels for 0%

profile of v1, /device:TPU:0, one launch (start us, length us, event | category | flops | bytes accessed | tf_op | source)
XLA Modules:
  0.0 358.9 jit_solution(8647165997242104566)
XLA Ops:
  7.2 0.0 copy-start
  7.2 0.0 all-gather.2.cloned.1.call-start
  7.2 0.7 all-gather.2.cloned.1.call-update
  7.9 4.1 %copy.20 = bf16[256,4096]{0,1:T(8,128)(2,1)} copy(bf16[256,4096]{1,0:T(8,128)(2,1)} %param.16) | data formatting | bytes 4194304 | tf_op args[7]
  12.0 4.1 %copy.21 = bf16[256,32,128]{2,0,1:T(8,128)(2,1)} copy(bf16[256,32,128]{0,2,1:T(8,128)(2,1)} %bitcast.73) | data formatting | bytes 4194304 | tf_op jit(solution)/shard_map/all_to_all | solution.py:100
  16.0 7.6 %all-to-all-start.1 = ((bf16[256,32,128]{2,0,1:T(8,128)(2,1)}), bf16[256,32,128]{2,0,1:T(8,128)(2,1)}, u32[]{:S(2)}, u32[]{:S(2)}) async-start(bf16[256,32,128]{2,0,1:T(8,128)(2,1)} %copy.21), calls=%async_computation.1 | async-start | bytes 4194304 | tf_op jit(solution)/shard_map/all_to_all | solution.py:100
  23.6 0.8 log_reduce_fusion
  24.4 0.1 log.15
  24.5 0.5 copy.18
  25.0 2.0 fusion.34
  27.0 0.4 copy.19
  27.4 0.1 slice_reduce_fusion
  27.5 0.1 subtract_exponential_fusion
  27.6 61.6 %all-gather.2.cloned.1.call-done = bf16[1024,4096]{1,0:T(8,128)(2,1)} async-done(((bf16[1024,128]{1,0:T(8,128)(2,1)}), bf16[1024,4096]{1,0:T(8,128)(2,1)}) %all-gather.2.cloned.1.call-update) | async-done | bytes 8388624 | tf_op jit(solution)/shard_map/all_gather | solution.py:37
  89.2 0.0 copy-start.4
  89.2 0.0 copy-start.5
  89.2 6.1 %convolution_convert_fusion.1 = bf16[1024,128]{1,0:T(8,128)(2,1)S(1)} fusion(bf16[1024,4096]{1,0:T(8,128)(2,1)} %all-gather.2.cloned.1.call-done, bf16[4096,128]{1,0:T(8,128)(2,1)} %param.13), kind=kOutput, calls=%fused_computation.14 | convolution fusion | flops 1073872896 | bytes 9699328 | tf_op jit(solution)/shard_map/dot_general | solution.py:41
  95.3 0.3 collective-permute-start.1
  95.6 0.0 copy-done.4
  95.6 0.0 copy-done.5
  95.6 2.3 fusion.9
  97.9 0.3 collective-permute-start
  98.3 0.0 copy-done
  98.3 2.3 convolution_convert_fusion
  100.6 0.0 collective-permute-done.1
  100.6 0.0 copy-start.2
  100.6 0.0 collective-permute-done
  100.6 0.7 copy-done.2
  101.3 0.0 copy-start.6
  101.3 1.6 convolution_bitcast_fusion
  102.9 4.4 %fusion.17 = (f32[32,32]{1,0:T(8,128)S(1)}, f32[32,32]{1,0:T(8,128)S(1)}, f32[32,1,256,32]{2,3,0,1:T(8,128)S(1)}) fusion(f32[32,1,256,32]{2,3,0,1:T(8,128)S(1)} %convolution_bitcast_fusion, f32[32,256,256]{2,1,0:T(8,128)} %param.11, bf16[32,32,128]{2,1,0:T(8,128)(2,1)S(1)} %bitcast.78, bf16[32,32,128]{2,1,0:T(8,128)(2,1)S(1)} %bitcast.80, pred[]{:T(512)S(6)} %eq.3, ...), kind=kOutput, calls=%fused_computation.23 | convolution fusion | flops 137885696 | bytes 11022337 | tf_op jit(solution)/shard_map/bngk,bkgv->bngv/dot_general | solution.py:67
  107.3 0.1 reduce_sum.25
  107.3 0.3 collective-permute-start.3
  107.6 0.1 reduce_sum.23
  107.7 0.5 collective-permute-start.2
  108.1 0.4 collective-permute-done.3
  108.5 0.5 collective-permute-done.2
  109.1 0.0 copy-done.6
  109.1 6.4 %fusion.16 = bf16[1024,256]{1,0:T(8,128)(2,1)S(1)} fusion(f32[32,1,256,32]{2,3,0,1:T(8,128)S(1)} %get-tuple-element.12, f32[256]{0:T(256)S(1)} %copy-done.6, f32[1024]{0:T(1024)S(1)} %bitcast.87, f32[1024]{0:T(1024)S(1)} %bitcast.88, bf16[1024,4096]{1,0:T(8,128)(2,1)} %all-gather.2.cloned.1.call-done, bf16[4096,256]{1,0:T(8,128)(2,1)} %param.15), kind=kOutput, calls=%fused_computation.20 | convolution fusion | flops 2149842944 | bytes 12067840 | tf_op jit(solution)/shard_map/dot_general | solution.py:41
  115.5 0.0 all-to-all-done.1
  115.5 6.0 %tile.2 = bf16[1024,32,256]{2,0,1:T(8,128)(2,1)} broadcast(bf16[1024,256]{1,0:T(8,128)(2,1)S(1)} %fusion.16), dimensions={0,2} | broadcast | bytes 17301504 | tf_op jit(solution)/shard_map/tile | solution.py:16
  121.5 5.7 %all-to-all-start = ((bf16[1024,32,256]{2,0,1:T(8,128)(2,1)}), bf16[1024,32,256]{2,0,1:T(8,128)(2,1)}, u32[]{:S(2)}, u32[]{:S(2)}) async-start(bf16[1024,32,256]{2,0,1:T(8,128)(2,1)} %tile.2), calls=%async_computation | async-start | bytes 33554432 | tf_op jit(solution)/shard_map/all_to_all | solution.py:15
  127.2 0.0 copy-start.3
  127.2 9.0 %copy.22 = f32[32,256,256]{1,2,0:T(8,128)} copy(f32[32,256,256]{2,1,0:T(8,128)} %param.11) | data formatting | bytes 16777216 | tf_op args[2]
  136.2 0.0 copy-done.3
  136.2 8.0 %fusion = f32[32,256,256]{1,2,0:T(8,128)} fusion(f32[32,256,256]{1,2,0:T(8,128)} %copy.22, f32[32]{0:T(128)S(1)} %exp.38, bf16[32,32,256]{2,1,0:T(8,128)(2,1)S(1)} %bitcast.75, f32[32,32]{1,0:T(8,128)S(1)} %get-tuple-element.10, bf16[32,32,128]{2,1,0:T(8,128)(2,1)S(1)} %bitcast.83, bf16[32,32,128]{2,1,0:T(8,128)(2,1)S(1)} %bitcast.85, pred[]{:T(512)S(6)} %eq.3), kind=kOutput, calls=%fused_computation.1 | convolution fusion | flops 141295616 | bytes 17830016 | tf_op jit(solution)/shard_map/bngk,bngv->bkgv/dot_general | solution.py:83
  144.2 0.0 copy-start.1
  144.2 9.1 %copy.23 = f32[32,256,256]{2,1,0:T(8,128)} copy(f32[32,256,256]{1,2,0:T(8,128)} %fusion) | data formatting | bytes 16777216
  153.3 187.2 %all-to-all-done = bf16[1024,32,256]{2,0,1:T(8,128)(2,1)} async-done(((bf16[1024,32,256]{2,0,1:T(8,128)(2,1)}), bf16[1024,32,256]{2,0,1:T(8,128)(2,1)}, u32[]{:S(2)}, u32[]{:S(2)}) %all-to-all-start) | async-done | bytes 16777248 | tf_op jit(solution)/shard_map/all_to_all | solution.py:15
  340.5 11.6 %fusion.10 = bf16[1024,128]{1,0:T(8,128)(2,1)} fusion(bf16[1024,32,256]{2,0,1:T(8,128)(2,1)} %all-to-all-done, bf16[256,32,128]{2,0,1:T(8,128)(2,1)} %all-to-all-done.1), kind=kOutput, calls=%fused_computation.15 | convolution fusion | flops 2147614720 | bytes 19136512 | tf_op jit(solution)/shard_map/dot_general | solution.py:102
  352.0 0.0 copy-done.1
  (3 shorter events, 0.0 us)
Async XLA Ops:
  7.2 91.1 %copy-start = (bf16[4096,256]{1,0:T(8,128)(2,1)S(1)}, bf16[4096,256]{1,0:T(8,128)(2,1)}, u32[]{:S(2)}) copy-start(bf16[4096,256]{1,0:T(8,128)(2,1)} %param.14) | copy-start | bytes 6291460
  7.2 82.0 %all-gather.2.cloned.1.call-start = ((), (), s32[]{:S(2)}) async-start(), calls=%async_computation.2 | async-start | bytes 8650752 | tf_op jit(solution)/shard_map/all_gather | solution.py:37
  16.0 99.5 %all-to-all-start.1 = ((bf16[256,32,128]{2,0,1:T(8,128)(2,1)}), bf16[256,32,128]{2,0,1:T(8,128)(2,1)}, u32[]{:S(2)}, u32[]{:S(2)}) async-start(bf16[256,32,128]{2,0,1:T(8,128)(2,1)} %copy.21), calls=%async_computation.1 | async-start | bytes 4194304 | tf_op jit(solution)/shard_map/all_to_all | solution.py:100
  89.2 6.4 %copy-start.4 = (bf16[1024,4096]{1,0:T(8,128)(2,1)S(1)}, bf16[1024,4096]{1,0:T(8,128)(2,1)}, u32[]{:S(2)}) copy-start(bf16[1024,4096]{1,0:T(8,128)(2,1)} %all-gather.2.cloned.1.call-done) | copy-start | bytes 25165828
  89.2 6.4 %copy-start.5 = (bf16[4096,128]{1,0:T(8,128)(2,1)S(1)}, bf16[4096,128]{1,0:T(8,128)(2,1)}, u32[]{:S(2)}) copy-start(bf16[4096,128]{1,0:T(8,128)(2,1)} %param.12) | copy-start | bytes 3145732
  95.3 5.4 %collective-permute-start.1 = (bf16[1024,1,128]{2,0,1:T(8,128)(2,1)S(1)}, bf16[1024,1,128]{2,0,1:T(8,128)(2,1)S(1)}, u32[]{:S(2)}, u32[]{:S(2)}) collective-permute-start(bf16[1024,1,128]{2,0,1:T(8,128)(2,1)S(1)} %bitcast.81), channel_id=1, source_target_pairs={{0,1},{1,0},{2,3},{3,2},{4,5},{5,4},{6,7},{7,6},{8,9},{9,8},{10,11... | collective-permute-start | bytes 786440 | tf_op jit(solution)/shard_map/ppermute | solution.py:21
  97.9 2.7 collective-permute-start
  100.6 0.7 copy-start.2
  101.3 7.7 %copy-start.6 = (f32[256]{0:T(256)S(1)}, f32[256]{0:T(256)}, u32[]{:S(2)}) copy-start(f32[256]{0:T(256)} %param.17) | copy-start | bytes 3076
  107.3 1.2 collective-permute-start.3
  107.7 1.4 collective-permute-start.2
  121.5 219.0 %all-to-all-start = ((bf16[1024,32,256]{2,0,1:T(8,128)(2,1)}), bf16[1024,32,256]{2,0,1:T(8,128)(2,1)}, u32[]{:S(2)}, u32[]{:S(2)}) async-start(bf16[1024,32,256]{2,0,1:T(8,128)(2,1)} %tile.2), calls=%async_computation | async-start | bytes 33554432 | tf_op jit(solution)/shard_map/all_to_all | solution.py:15
  127.2 9.0 %copy-start.3 = (bf16[1024,1,128]{2,0,1:T(8,128)(2,1)S(1)}, bf16[1024,1,128]{2,0,1:T(8,128)(2,1)}, u32[]{:S(2)}) copy-start(bf16[1024,1,128]{2,0,1:T(8,128)(2,1)} %copy-done.2) | copy-start | bytes 786436
  144.2 207.8 %copy-start.1 = (bf16[4096,256]{1,0:T(8,128)(2,1)S(1)}, bf16[4096,256]{1,0:T(8,128)(2,1)}, u32[]{:S(2)}) copy-start(bf16[4096,256]{1,0:T(8,128)(2,1)} %param.14) | copy-start | bytes 6291460
Sparse Core Ops, SparseCore 0:
  10.2 78.9 all-gather.1
